TPU v7x, 32 devices: a whole 2x2x4 slice. The times are simulated.
32 devices in a mesh: job: 2 (over core), replica: 4 (over z), model: 4 (over y, x).
Axes of the slice: x: 2, y: 2, z: 4, core: 2. Of those that a mesh axis runs over, the one named last changes fastest.
Arguments:
- grad_query: float32 [8, 1024, 1024], P(('job', 'replica'), None, 'model'), parts along dimension 0, may hold values from -0.875 to 0.875
- grad_key: float32 [8, 1024, 1024], P(('job', 'replica'), None, 'model'), parts along dimension 0, may hold values from -0.875 to 0.875
- grad_value: float32 [8, 1024, 1024], P(('job', 'replica'), None, 'model'), parts along dimension 0, may hold values from -0.875 to 0.875
- grad_mixed: float32 [8, 1024, 1024], P(('job', 'replica'), 'model'), parts along dimension 0, may hold values from -0.875 to 0.875
- grad_norm: float32 [8, 1024], P(('job', 'replica')), parts along dimension 0, may hold values from -8 to 8
- weight_query: float32 [2048, 1024], P(('job', 'replica'), 'model'), parts along dimension 0, may hold values from -0.25 to 0.25
- weight_key: float32 [2048, 1024], P(('job', 'replica'), 'model'), parts along dimension 0, may hold values from -0.25 to 0.25
- weight_value: float32 [2048, 1024], P(('job', 'replica'), 'model'), parts along dimension 0, may hold values from -0.25 to 0.25
- weight_mixed: float32 [2048, 1024], P(('job', 'model'), 'replica'), parts along dimension 0, may hold values from -0.25 to 0.25
- weight_norm: float32 [2048], P(('job', 'replica')), parts along dimension 0, may hold values from 0.25 to 1.75
- moment_query: float32 [2048, 1024], P(('job', 'replica'), 'model'), parts along dimension 0, may hold values from -0.1875 to 0.1875
- moment_key: float32 [2048, 1024], P(('job', 'replica'), 'model'), parts along dimension 0, may hold values from -0.1875 to 0.1875
- moment_value: float32 [2048, 1024], P(('job', 'replica'), 'model'), parts along dimension 0, may hold values from -0.1875 to 0.1875
- moment_mixed: float32 [2048, 1024], P(('job', 'model'), 'replica'), parts along dimension 0, may hold values from -0.1875 to 0.1875
- moment_norm: float32 [2048], P(('job', 'replica')), parts along dimension 0, may hold values from -1.75 to 1.75
Outputs:
- copy_query: bfloat16 [2048, 1024], P('job', 'model'), parts along dimension 0
- copy_key: bfloat16 [2048, 1024], P('job', 'model'), parts along dimension 0
- copy_value: bfloat16 [2048, 1024], P('job', 'model'), parts along dimension 0
- copy_mixed: bfloat16 [2048, 1024], P(('job', 'model')), parts along dimension 0
- copy_norm: bfloat16 [2048], P('job'), parts along dimension 0
- new_query: float32 [2048, 1024], P(('job', 'replica'), 'model'), parts along dimension 0
- new_key: float32 [2048, 1024], P(('job', 'replica'), 'model'), parts along dimension 0
- new_value: float32 [2048, 1024], P(('job', 'replica'), 'model'), parts along dimension 0
- new_mixed: float32 [2048, 1024], P(('job', 'model'), 'replica'), parts along dimension 0
- new_norm: float32 [2048], P(('job', 'replica')), parts along dimension 0
- state_new_query: float32 [2048, 1024], P(('job', 'replica'), 'model'), parts along dimension 0
- state_new_key: float32 [2048, 1024], P(('job', 'replica'), 'model'), parts along dimension 0
- state_new_value: float32 [2048, 1024], P(('job', 'replica'), 'model'), parts along dimension 0
- state_new_mixed: float32 [2048, 1024], P(('job', 'model'), 'replica'), parts along dimension 0
- state_new_norm: float32 [2048], P(('job', 'replica')), parts along dimension 0
There are 2 independent parts, one for each index of `job`. A program takes and returns all parts, laid end to end along the dimension named above; each array names one. Nothing has to cross between parts.
All inputs are finite; a program needn't handle non-finite values.
Results may differ from a plain program's by a relative error of at most 0.0004.
Values may be sent and summed in bfloat16 or wider, within the bound.
No kernel may reach another device: no remote copies, remote signals or barrier semaphores. Data moves between devices by JAX's collectives and lax.ppermute only.
A program may use at most 64 MiB of HBM per device.

v0:
```python
import jax
import jax.numpy as jnp
from jax import lax
from jax.sharding import PartitionSpec as P

learn_rate = 0.5
hold_rate = 0.9


def local(
    grad_query,
    grad_key,
    grad_value,
    grad_mixed,
    grad_norm,
    weight_query,
    weight_key,
    weight_value,
    weight_mixed,
    weight_norm,
    moment_query,
    moment_key,
    moment_value,
    moment_mixed,
    moment_norm,
):
    mean_query, mean_key, mean_value, mean_mixed = (
        lax.psum_scatter(grad_query[0], "replica", scatter_dimension=0, tiled=True),
        lax.psum_scatter(grad_key[0], "replica", scatter_dimension=0, tiled=True),
        lax.psum_scatter(grad_value[0], "replica", scatter_dimension=0, tiled=True),
        lax.psum_scatter(grad_mixed[0], "replica", scatter_dimension=1, tiled=True),
    )
    whole_norm = lax.psum(grad_norm[0], "replica")
    place = lax.axis_index("replica")
    mean_norm = lax.dynamic_slice_in_dim(
        whole_norm, place * weight_norm.shape[0], weight_norm.shape[0]
    )
    mean_rate = lax.axis_size("replica") ** (-0.5)
    mean_query = mean_query * mean_rate
    mean_key = mean_key * mean_rate
    mean_value = mean_value * mean_rate
    mean_mixed = mean_mixed * mean_rate
    mean_norm = mean_norm * mean_rate
    (
        own_query,
        own_key,
        own_value,
        own_mixed,
        slope_query_norm,
        slope_key_norm,
        slope_value_norm,
        slope_mixed_norm,
    ) = lax.psum(
        (
            jnp.sum(weight_query * weight_query, axis=1, keepdims=True),
            jnp.sum(weight_key * weight_key, axis=1, keepdims=True),
            jnp.sum(weight_value * weight_value, axis=1, keepdims=True),
            jnp.sum(weight_mixed * weight_mixed, axis=0, keepdims=True),
            jnp.sum(mean_query * mean_query, axis=1, keepdims=True),
            jnp.sum(mean_key * mean_key, axis=1, keepdims=True),
            jnp.sum(mean_value * mean_value, axis=1, keepdims=True),
            jnp.sum(mean_mixed * mean_mixed, axis=0, keepdims=True),
        ),
        "model",
    )
    mean_query = mean_query * (jnp.sqrt(own_query) * lax.rsqrt(slope_query_norm + 1e-06))
    mean_key = mean_key * (jnp.sqrt(own_key) * lax.rsqrt(slope_key_norm + 1e-06))
    mean_value = mean_value * (jnp.sqrt(own_value) * lax.rsqrt(slope_value_norm + 1e-06))
    mean_mixed = mean_mixed * (jnp.sqrt(own_mixed) * lax.rsqrt(slope_mixed_norm + 1e-06))
    state_new_query = hold_rate * moment_query + mean_query
    new_query = weight_query - learn_rate * state_new_query
    state_new_key = hold_rate * moment_key + mean_key
    new_key = weight_key - learn_rate * state_new_key
    state_new_value = hold_rate * moment_value + mean_value
    new_value = weight_value - learn_rate * state_new_value
    state_new_mixed = hold_rate * moment_mixed + mean_mixed
    new_mixed = weight_mixed - learn_rate * state_new_mixed
    state_new_norm = hold_rate * moment_norm + mean_norm
    new_norm = weight_norm - learn_rate * state_new_norm
    copy_query, copy_key, copy_value, copy_mixed, copy_norm = (
        lax.all_gather(new_query.astype(jnp.bfloat16), "replica", axis=0, tiled=True),
        lax.all_gather(new_key.astype(jnp.bfloat16), "replica", axis=0, tiled=True),
        lax.all_gather(new_value.astype(jnp.bfloat16), "replica", axis=0, tiled=True),
        lax.all_gather(new_mixed.astype(jnp.bfloat16), "replica", axis=1, tiled=True),
        lax.all_gather(new_norm.astype(jnp.bfloat16), "replica", axis=0, tiled=True),
    )
    return (
        copy_query,
        copy_key,
        copy_value,
        copy_mixed,
        copy_norm,
        new_query,
        new_key,
        new_value,
        new_mixed,
        new_norm,
        state_new_query,
        state_new_key,
        state_new_value,
        state_new_mixed,
        state_new_norm,
    )


def solution(mesh):
    placed = (
        P(("job", "replica"), None, "model"),
        P(("job", "replica"), None, "model"),
        P(("job", "replica"), None, "model"),
        P(("job", "replica"), "model", None),
        P(("job", "replica"), None),
        P(("job", "replica"), "model"),
        P(("job", "replica"), "model"),
        P(("job", "replica"), "model"),
        P(("job", "model"), "replica"),
        P(("job", "replica")),
        P(("job", "replica"), "model"),
        P(("job", "replica"), "model"),
        P(("job", "replica"), "model"),
        P(("job", "model"), "replica"),
        P(("job", "replica")),
    )
    return jax.shard_map(
        local,
        mesh=mesh,
        in_specs=placed,
        out_specs=(
            P("job", "model"),
            P("job", "model"),
            P("job", "model"),
            P(("job", "model"), None),
            P("job"),
            P(("job", "replica"), "model"),
            P(("job", "replica"), "model"),
            P(("job", "replica"), "model"),
            P(("job", "model"), "replica"),
            P(("job", "replica")),
            P(("job", "replica"), "model"),
            P(("job", "replica"), "model"),
            P(("job", "replica"), "model"),
            P(("job", "model"), "replica"),
            P(("job", "replica")),
        ),
        check_vma=False,
    )
```

profile of v0, /device:TPU:0, one launch (start us, length us, event | category | flops | bytes accessed | tf_op | source)
XLA Modules:
  0.0 210.1 jit_solution(8399502176376450542)
XLA Ops:
  10.1 13.5 %psum.71 = f32[1024]{0:T(1024)S(1)} all-reduce(f32[1024]{0:T(1024)S(1)} %bitcast.36), channel_id=1, replica_groups=mesh['job'=2,'replica'=4,'model'=4] {'replica'}, use_global_device_ids=true, to_apply=%region_20.0 | all-reduce | flops 1024 | bytes 8192 | tf_op jit(solution)/shard_map/psum | solution.py:33
  24.3 7.7 %all-gather = bf16[4,1,256]{2,1,0:T(2,128)(2,1)S(1)} all-gather(bf16[1,1,256]{2,1,0:T(2,128)(2,1)S(1)} %reshape.38), channel_id=1, replica_groups=mesh['job'=2,'replica'=4,'model'=4] {'replica'}, dimensions={0}, use_global_device_ids=true | all-gather | bytes 2560 | tf_op jit(solution)/shard_map/all_gather | solution.py:85
  32.8 0.8 copy-done
  33.8 6.6 %reduce-scatter.9.cloned.1.call-done = f32[256,256]{1,0:T(8,128)} async-done(((f32[1024,256]{1,0:T(8,128)}), f32[256,256]{1,0:T(8,128)}) %reduce-scatter.9.cloned.1.call-update) | async-done | bytes 262160 | tf_op jit(solution)/shard_map/reduce_scatter | solution.py:30
  40.4 1.1 multiply_reduce_fusion.2
  41.5 27.1 %reduce-scatter.11.cloned.1.call-done = f32[256,256]{1,0:T(8,128)} async-done(((f32[256,1024]{1,0:T(8,128)}), f32[256,256]{1,0:T(8,128)}) %reduce-scatter.11.cloned.1.call-update) | async-done | bytes 262160 | tf_op jit(solution)/shard_map/reduce_scatter | solution.py:31
  68.6 1.0 multiply_reduce_fusion
  69.6 27.1 %reduce-scatter.5.cloned.1.call-done = f32[256,256]{1,0:T(8,128)} async-done(((f32[1024,256]{1,0:T(8,128)}), f32[256,256]{1,0:T(8,128)}) %reduce-scatter.5.cloned.1.call-update) | async-done | bytes 262160 | tf_op jit(solution)/shard_map/reduce_scatter | solution.py:28
  96.7 1.1 multiply_reduce_fusion.6
  97.7 26.9 %reduce-scatter.7.cloned.1.call-done = f32[256,256]{1,0:T(8,128)} async-done(((f32[1024,256]{1,0:T(8,128)}), f32[256,256]{1,0:T(8,128)}) %reduce-scatter.7.cloned.1.call-update) | async-done | bytes 262160 | tf_op jit(solution)/shard_map/reduce_scatter | solution.py:29
  124.7 1.1 multiply_reduce_fusion.4
  125.8 10.0 %all-reduce = (f32[256,1]{0,1:T(1,128)S(1)}, f32[256,1]{0,1:T(1,128)S(1)}, f32[256,1]{0,1:T(1,128)S(1)}, f32[256,1]{0,1:T(1,128)S(1)}, f32[256,1]{0,1:T(1,128)S(...) all-reduce(f32[256,1]{0,1:T(1,128)S(1)} %bitcast.34, ...), channel_id=1, replica_groups=mesh['job'=2,'replica'=4,'model'=4] {'model'}, use_global_device_ids=true, to_apply=%region_4.0 | all-reduce | flops 2048 | bytes 16384 | tf_op jit(solution)/shard_map/psum | solution.py:53
  135.8 0.9 fusion.3
  136.7 14.8 %all_gather.16 = bf16[1024,256]{1,0:T(8,128)(2,1)S(1)} all-gather(bf16[256,256]{1,0:T(8,128)(2,1)S(1)} %get-tuple-element.32), channel_id=1, replica_groups=mesh['job'=2,'replica'=4,'model'=4] {'replica'}, dimensions={0}, use_global_device_ids=true | all-gather | bytes 655360 | tf_op jit(solution)/shard_map/all_gather | solution.py:82
  151.5 0.9 fusion.2
  152.4 15.3 %all_gather.17 = bf16[1024,256]{1,0:T(8,128)(2,1)S(1)} all-gather(bf16[256,256]{1,0:T(8,128)(2,1)S(1)} %get-tuple-element.29), channel_id=1, replica_groups=mesh['job'=2,'replica'=4,'model'=4] {'replica'}, dimensions={0}, use_global_device_ids=true | all-gather | bytes 655360 | tf_op jit(solution)/shard_map/all_gather | solution.py:83
  167.8 0.8 fusion.1
  168.6 16.1 %all_gather.18 = bf16[256,1024]{1,0:T(8,128)(2,1)S(1)} all-gather(bf16[256,256]{1,0:T(8,128)(2,1)S(1)} %get-tuple-element.26), channel_id=1, replica_groups=mesh['job'=2,'replica'=4,'model'=4] {'replica'}, dimensions={1}, use_global_device_ids=true | all-gather | bytes 655360 | tf_op jit(solution)/shard_map/all_gather | solution.py:84
  184.7 0.9 fusion.4
  185.7 14.8 %all_gather.15 = bf16[1024,256]{1,0:T(8,128)(2,1)S(1)} all-gather(bf16[256,256]{1,0:T(8,128)(2,1)S(1)} %get-tuple-element.35), channel_id=1, replica_groups=mesh['job'=2,'replica'=4,'model'=4] {'replica'}, dimensions={0}, use_global_device_ids=true | all-gather | bytes 655360 | tf_op jit(solution)/shard_map/all_gather | solution.py:81
  200.4 0.8 copy.35
  201.2 0.8 copy.36
  202.0 0.8 copy.37
  202.8 0.8 copy.38
  (48 shorter events, 4.6 us)
Async XLA Ops:
  7.2 33.2 %reduce-scatter.9.cloned.1.call-start = ((), (), s32[]{:S(2)}) async-start(), calls=%async_computation.6 | async-start | bytes 1310720 | tf_op jit(solution)/shard_map/reduce_scatter | solution.py:30
  7.9 60.6 %reduce-scatter.11.cloned.1.call-start = ((), (), s32[]{:S(2)}) async-start(), calls=%async_computation.7 | async-start | bytes 1310720 | tf_op jit(solution)/shard_map/reduce_scatter | solution.py:31
  8.7 88.0 %reduce-scatter.5.cloned.1.call-start = ((), (), s32[]{:S(2)}) async-start(), calls=%async_computation.4 | async-start | bytes 1310720 | tf_op jit(solution)/shard_map/reduce_scatter | solution.py:28
  9.4 115.2 %reduce-scatter.7.cloned.1.call-start = ((), (), s32[]{:S(2)}) async-start(), calls=%async_computation.5 | async-start | bytes 1310720 | tf_op jit(solution)/shard_map/reduce_scatter | solution.py:29
  9.4 0.7 copy-start.12
  9.5 14.1 %copy-start.13 = (f32[256]{0:T(256)S(1)}, f32[256]{0:T(256)}, u32[]{:S(2)}) copy-start(f32[256]{0:T(256)} %param.24) | copy-start | bytes 3076
  9.5 14.1 %copy-start.14 = (f32[256]{0:T(256)S(1)}, f32[256]{0:T(256)}, u32[]{:S(2)}) copy-start(f32[256]{0:T(256)} %param.29) | copy-start | bytes 3076
  9.5 23.1 %copy-start.3 = (f32[256,256]{1,0:T(8,128)S(1)}, f32[256,256]{1,0:T(8,128)}, u32[]{:S(2)}) copy-start(f32[256,256]{1,0:T(8,128)} %param.20) | copy-start | bytes 786436
  10.0 22.7 %copy-start.2 = (f32[256,256]{1,0:T(8,128)S(1)}, f32[256,256]{1,0:T(8,128)}, u32[]{:S(2)}) copy-start(f32[256,256]{1,0:T(8,128)} %param.23) | copy-start | bytes 786436
  32.6 1.0 copy-start
  32.7 1.0 copy-start.1
  69.6 66.2 %copy-start.8 = (f32[256,256]{1,0:T(8,128)S(1)}, f32[256,256]{1,0:T(8,128)}, u32[]{:S(2)}) copy-start(f32[256,256]{1,0:T(8,128)} %param.26) | copy-start | bytes 786436
  124.7 11.2 %copy-start.7 = (f32[256,256]{1,0:T(8,128)S(1)}, f32[256,256]{1,0:T(8,128)}, u32[]{:S(2)}) copy-start(f32[256,256]{1,0:T(8,128)} %reduce-scatter.7.cloned.1.call-done) | copy-start | bytes 786436
  136.7 14.8 %copy-start.6 = (f32[256,256]{1,0:T(8,128)S(1)}, f32[256,256]{1,0:T(8,128)}, u32[]{:S(2)}) copy-start(f32[256,256]{1,0:T(8,128)} %reduce-scatter.9.cloned.1.call-done) | copy-start | bytes 786436
  136.7 14.8 %copy-start.9 = (f32[256,256]{1,0:T(8,128)S(1)}, f32[256,256]{1,0:T(8,128)}, u32[]{:S(2)}) copy-start(f32[256,256]{1,0:T(8,128)} %param.27) | copy-start | bytes 786436
  152.4 15.3 %copy-start.5 = (f32[256,256]{1,0:T(8,128)S(1)}, f32[256,256]{1,0:T(8,128)}, u32[]{:S(2)}) copy-start(f32[256,256]{1,0:T(8,128)} %reduce-scatter.11.cloned.1.call-done) | copy-start | bytes 786436
  152.4 15.4 %copy-start.10 = (f32[256,256]{1,0:T(8,128)S(1)}, f32[256,256]{1,0:T(8,128)}, u32[]{:S(2)}) copy-start(f32[256,256]{1,0:T(8,128)} %param.28) | copy-start | bytes 786436
  168.6 16.1 %copy-start.4 = (f32[256,256]{1,0:T(8,128)S(1)}, f32[256,256]{1,0:T(8,128)}, u32[]{:S(2)}) copy-start(f32[256,256]{1,0:T(8,128)} %reduce-scatter.5.cloned.1.call-done) | copy-start | bytes 786436
  168.6 16.1 %copy-start.11 = (f32[256,256]{1,0:T(8,128)S(1)}, f32[256,256]{1,0:T(8,128)}, u32[]{:S(2)}) copy-start(f32[256,256]{1,0:T(8,128)} %param.25) | copy-start | bytes 786436
Sparse Core Ops, SparseCore 0:
  10.3 30.1 reduce-scatter.8
  42.7 25.7 reduce-scatter.10
  70.9 25.7 reduce-scatter.4
  98.8 25.7 reduce-scatter.6
where the time goes:
time: 210 us
  blocking collectives  92.1 us (44%)
  waiting for transfers between devices  90.2 us (43%)
  between operations  14 us (7%)
  other arithmetic  8.91 us (4%)
  local copies, waits for them, and re-layouts  4.75 us (2%)
    reduce_scatter x1, waiting for transfers between devices, local(): lax.psum_scatter(grad_query[0], 'replica', scatter_dimension=0, tiled=True)  27.1 us
    reduce_scatter x1, waiting for transfers between devices, local(): lax.psum_scatter(grad_mixed[0], 'replica', scatter_dimension=1, tiled=True)  27.1 us
    reduce_scatter x1, waiting for transfers between devices, local(): lax.psum_scatter(grad_key[0], 'replica', scatter_dimension=0, tiled=True)  26.9 us
    all_gather x1, blocking collectives, local(): lax.all_gather(new_mixed.astype(jnp.bfloat16), 'replica', axis=1, tiled=T...  16.1 us
    all_gather x1, blocking collectives, local(): lax.all_gather(new_value.astype(jnp.bfloat16), 'replica', axis=0, tiled=T...  15.3 us
    all_gather x1, blocking collectives, local(): lax.all_gather(new_key.astype(jnp.bfloat16), 'replica', axis=0, tiled=True)  14.8 us
    all_gather x1, blocking collectives, local(): lax.all_gather(new_query.astype(jnp.bfloat16), 'replica', axis=0, tiled=T...  14.8 us
    psum x1, blocking collectives, local(): whole_norm = lax.psum(grad_norm[0], 'replica')  13.5 us
  transfers between devices with their start and end apart: 4, of which 4 were waited for; matrix products, arithmetic and copies ran while one was open for 2% of the time, Pallas kernels for 0%

commit v1 on v0

--- a/solution.py
+++ b/solution.py
@@ -5,6 +5,19 @@
 
 learn_rate = 0.5
 hold_rate = 0.9
+
+
+def collect(shard, axis, dim):
+    ways = lax.axis_size(axis)
+    up = [(d, (d + 1) % ways) for d in range(ways)]
+    down = [(d, (d - 1) % ways) for d in range(ways)]
+    earlier, later = ([shard], [shard])
+    for _ in range(ways // 2):
+        earlier.append(lax.ppermute(earlier[-1], axis, up))
+    for _ in range((ways - 1) // 2):
+        later.append(lax.ppermute(later[-1], axis, down))
+    line = jnp.concatenate([*earlier[::-1], *later[1:]], axis=dim)
+    return jnp.roll(line, (lax.axis_index(axis) - ways // 2) * shard.shape[dim], axis=dim)
 
 
 def local(
@@ -78,7 +91,7 @@
     state_new_norm = hold_rate * moment_norm + mean_norm
     new_norm = weight_norm - learn_rate * state_new_norm
     copy_query, copy_key, copy_value, copy_mixed, copy_norm = (
-        lax.all_gather(new_query.astype(jnp.bfloat16), "replica", axis=0, tiled=True),
+        collect(new_query.astype(jnp.bfloat16), "replica", 0),
         lax.all_gather(new_key.astype(jnp.bfloat16), "replica", axis=0, tiled=True),
         lax.all_gather(new_value.astype(jnp.bfloat16), "replica", axis=0, tiled=True),
         lax.all_gather(new_mixed.astype(jnp.bfloat16), "replica", axis=1, tiled=True),

time: 210 us -> 201 us (0.957)
  blocking collectives: 92.1 us -> 79.1 us
  starting transfers between devices: 0.15 us -> 3.98 us
    all_gather x1 -> x0, blocking collectives: 14.8 us -> none  [local(): lax.all_gather(new_query.astype(jnp.bfloat16), 'replica', axis=0, tiled=T...]
    ppermute x0 -> x3, starting transfers between devices: none -> 3.83 us  [the longest x1 3.82 us: collect(): later.append(lax.ppermute(later[-1], axis, down))]
    unnamed x36 -> x42, local copies, waits for them, and re-layouts: 4.75 us -> 4.02 us
  transfers between devices with their start and end apart: 4 -> 7, of which waited for: 4 -> 4; matrix products, arithmetic and copies ran while one was open for 2% -> 4% of each run, Pallas kernels for 0% -> 0%
where the time goes in v1:
time: 201 us
  waiting for transfers between devices  90.2 us (45%)
  blocking collectives  79.1 us (39%)
  between operations  14.1 us (7%)
  other arithmetic  8.91 us (4%)
  local copies, waits for them, and re-layouts  4.86 us (2%)
  starting transfers between devices  3.98 us (2%)
    reduce_scatter x1, waiting for transfers between devices, local(): lax.psum_scatter(grad_query[0], 'replica', scatter_dimension=0, tiled=True)  27.1 us
    reduce_scatter x1, waiting for transfers between devices, local(): lax.psum_scatter(grad_mixed[0], 'replica', scatter_dimension=1, tiled=True)  27.1 us
    reduce_scatter x1, waiting for transfers between devices, local(): lax.psum_scatter(grad_key[0], 'replica', scatter_dimension=0, tiled=True)  26.8 us
    all_gather x1, blocking collectives, local(): lax.all_gather(new_mixed.astype(jnp.bfloat16), 'replica', axis=1, tiled=T...  16.6 us
    all_gather x1, blocking collectives, local(): lax.all_gather(new_value.astype(jnp.bfloat16), 'replica', axis=0, tiled=T...  16.1 us
    all_gather x1, blocking collectives, local(): lax.all_gather(new_key.astype(jnp.bfloat16), 'replica', axis=0, tiled=True)  15.2 us
    psum x1, blocking collectives, local(): whole_norm = lax.psum(grad_norm[0], 'replica')  13.5 us
    psum x1, blocking collectives, local(): lax.psum((jnp.sum(weight_query * weight_query, axis=1, keepdims=True), jn...  9.98 us
  transfers between devices with their start and end apart: 7, of which 4 were waited for; matrix products, arithmetic and copies ran while one was open for 4% of the time, Pallas kernels for 0%

profile of v1, /device:TPU:0, one launch (start us, length us, event | category | flops | bytes accessed | tf_op | source)
XLA Modules:
  0.0 201.1 jit_solution(10303013348562320321)
XLA Ops:
  10.1 13.5 %psum.71 = f32[1024]{0:T(1024)S(1)} all-reduce(f32[1024]{0:T(1024)S(1)} %bitcast.36), channel_id=1, replica_groups=mesh['job'=2,'replica'=4,'model'=4] {'replica'}, use_global_device_ids=true, to_apply=%region_20.0 | all-reduce | flops 1024 | bytes 8192 | tf_op jit(solution)/shard_map/psum | solution.py:46
  24.3 7.7 %all-gather = bf16[4,1,256]{2,1,0:T(2,128)(2,1)S(1)} all-gather(bf16[1,1,256]{2,1,0:T(2,128)(2,1)S(1)} %reshape.38), channel_id=1, replica_groups=mesh['job'=2,'replica'=4,'model'=4] {'replica'}, dimensions={0}, use_global_device_ids=true | all-gather | bytes 2560 | tf_op jit(solution)/shard_map/all_gather | solution.py:98
  32.8 0.8 copy-done.1
  33.8 6.6 %reduce-scatter.9.cloned.1.call-done = f32[256,256]{1,0:T(8,128)} async-done(((f32[1024,256]{1,0:T(8,128)}), f32[256,256]{1,0:T(8,128)}) %reduce-scatter.9.cloned.1.call-update) | async-done | bytes 262160 | tf_op jit(solution)/shard_map/reduce_scatter | solution.py:43
  40.4 1.1 multiply_reduce_fusion.2
  41.5 27.1 %reduce-scatter.11.cloned.1.call-done = f32[256,256]{1,0:T(8,128)} async-done(((f32[256,1024]{1,0:T(8,128)}), f32[256,256]{1,0:T(8,128)}) %reduce-scatter.11.cloned.1.call-update) | async-done | bytes 262160 | tf_op jit(solution)/shard_map/reduce_scatter | solution.py:44
  68.6 1.0 multiply_reduce_fusion
  69.6 27.1 %reduce-scatter.5.cloned.1.call-done = f32[256,256]{1,0:T(8,128)} async-done(((f32[1024,256]{1,0:T(8,128)}), f32[256,256]{1,0:T(8,128)}) %reduce-scatter.5.cloned.1.call-update) | async-done | bytes 262160 | tf_op jit(solution)/shard_map/reduce_scatter | solution.py:41
  96.7 1.1 multiply_reduce_fusion.6
  97.8 26.8 %reduce-scatter.7.cloned.1.call-done = f32[256,256]{1,0:T(8,128)} async-done(((f32[1024,256]{1,0:T(8,128)}), f32[256,256]{1,0:T(8,128)}) %reduce-scatter.7.cloned.1.call-update) | async-done | bytes 262160 | tf_op jit(solution)/shard_map/reduce_scatter | solution.py:42
  124.7 1.1 multiply_reduce_fusion.4
  125.7 10.0 %all-reduce = (f32[256,1]{0,1:T(1,128)S(1)}, f32[256,1]{0,1:T(1,128)S(1)}, f32[256,1]{0,1:T(1,128)S(1)}, f32[256,1]{0,1:T(1,128)S(1)}, f32[256,1]{0,1:T(1,128)S(...) all-reduce(f32[256,1]{0,1:T(1,128)S(1)} %bitcast.34, ...), channel_id=1, replica_groups=mesh['job'=2,'replica'=4,'model'=4] {'model'}, use_global_device_ids=true, to_apply=%region_4.0 | all-reduce | flops 2048 | bytes 16384 | tf_op jit(solution)/shard_map/psum | solution.py:66
  135.8 0.9 fusion.4
  136.7 3.8 %collective-permute-start.2 = (bf16[256,256]{1,0:T(8,128)(2,1)S(1)}, bf16[256,256]{1,0:T(8,128)(2,1)S(1)}, u32[]{:S(2)}, u32[]{:S(2)}) collective-permute-start(bf16[256,256]{1,0:T(8,128)(2,1)S(1)} %get-tuple-element.35), channel_id=1, source_target_pairs={{0,12},{4,0},{8,4},{12,8},{1,13},{5,1},{9,5},{13,9},{2,14},{6,2},{... | collective-permute-start | bytes 393224 | tf_op jit(solution)/shard_map/ppermute | solution.py:18
  140.5 0.9 fusion.3
  141.4 15.2 %all_gather.12 = bf16[1024,256]{1,0:T(8,128)(2,1)S(1)} all-gather(bf16[256,256]{1,0:T(8,128)(2,1)S(1)} %get-tuple-element.32), channel_id=1, replica_groups=mesh['job'=2,'replica'=4,'model'=4] {'replica'}, dimensions={0}, use_global_device_ids=true | all-gather | bytes 655360 | tf_op jit(solution)/shard_map/all_gather | solution.py:95
  156.7 0.9 fusion.2
  157.6 16.1 %all_gather.13 = bf16[1024,256]{1,0:T(8,128)(2,1)S(1)} all-gather(bf16[256,256]{1,0:T(8,128)(2,1)S(1)} %get-tuple-element.29), channel_id=1, replica_groups=mesh['job'=2,'replica'=4,'model'=4] {'replica'}, dimensions={0}, use_global_device_ids=true | all-gather | bytes 655360 | tf_op jit(solution)/shard_map/all_gather | solution.py:96
  173.7 0.8 fusion.1
  174.6 16.6 %all_gather.14 = bf16[256,1024]{1,0:T(8,128)(2,1)S(1)} all-gather(bf16[256,256]{1,0:T(8,128)(2,1)S(1)} %get-tuple-element.26), channel_id=1, replica_groups=mesh['job'=2,'replica'=4,'model'=4] {'replica'}, dimensions={1}, use_global_device_ids=true | all-gather | bytes 655360 | tf_op jit(solution)/shard_map/all_gather | solution.py:97
  191.3 0.8 constant_dynamic-slice_fusion
  192.2 0.8 copy.41
  193.0 0.8 copy.42
  193.7 0.8 copy.43
  (61 shorter events, 4.7 us)
Async XLA Ops:
  7.2 33.2 %reduce-scatter.9.cloned.1.call-start = ((), (), s32[]{:S(2)}) async-start(), calls=%async_computation.6 | async-start | bytes 1310720 | tf_op jit(solution)/shard_map/reduce_scatter | solution.py:43
  7.9 60.6 %reduce-scatter.11.cloned.1.call-start = ((), (), s32[]{:S(2)}) async-start(), calls=%async_computation.7 | async-start | bytes 1310720 | tf_op jit(solution)/shard_map/reduce_scatter | solution.py:44
  8.7 88.0 %reduce-scatter.5.cloned.1.call-start = ((), (), s32[]{:S(2)}) async-start(), calls=%async_computation.4 | async-start | bytes 1310720 | tf_op jit(solution)/shard_map/reduce_scatter | solution.py:41
  9.4 115.2 %reduce-scatter.7.cloned.1.call-start = ((), (), s32[]{:S(2)}) async-start(), calls=%async_computation.5 | async-start | bytes 1310720 | tf_op jit(solution)/shard_map/reduce_scatter | solution.py:42
  9.4 0.7 copy-start.12
  9.5 14.1 %copy-start.13 = (f32[256]{0:T(256)S(1)}, f32[256]{0:T(256)}, u32[]{:S(2)}) copy-start(f32[256]{0:T(256)} %param.24) | copy-start | bytes 3076
  9.5 14.1 %copy-start.14 = (f32[256]{0:T(256)S(1)}, f32[256]{0:T(256)}, u32[]{:S(2)}) copy-start(f32[256]{0:T(256)} %param.29) | copy-start | bytes 3076
  9.5 23.1 %copy-start = (f32[256,256]{1,0:T(8,128)S(1)}, f32[256,256]{1,0:T(8,128)}, u32[]{:S(2)}) copy-start(f32[256,256]{1,0:T(8,128)} %param.20) | copy-start | bytes 786436
  10.0 22.7 %copy-start.3 = (f32[256,256]{1,0:T(8,128)S(1)}, f32[256,256]{1,0:T(8,128)}, u32[]{:S(2)}) copy-start(f32[256,256]{1,0:T(8,128)} %param.23) | copy-start | bytes 786436
  32.6 1.0 copy-start.1
  32.7 1.0 copy-start.2
  69.6 66.2 %copy-start.8 = (f32[256,256]{1,0:T(8,128)S(1)}, f32[256,256]{1,0:T(8,128)}, u32[]{:S(2)}) copy-start(f32[256,256]{1,0:T(8,128)} %param.25) | copy-start | bytes 786436
  96.7 39.1 %copy-start.7 = (f32[256,256]{1,0:T(8,128)S(1)}, f32[256,256]{1,0:T(8,128)}, u32[]{:S(2)}) copy-start(f32[256,256]{1,0:T(8,128)} %reduce-scatter.5.cloned.1.call-done) | copy-start | bytes 786436
  135.7 4.8 %copy-start.6 = (f32[256,256]{1,0:T(8,128)S(1)}, f32[256,256]{1,0:T(8,128)}, u32[]{:S(2)}) copy-start(f32[256,256]{1,0:T(8,128)} %reduce-scatter.7.cloned.1.call-done) | copy-start | bytes 786436
  135.8 4.8 %copy-start.9 = (f32[256,256]{1,0:T(8,128)S(1)}, f32[256,256]{1,0:T(8,128)}, u32[]{:S(2)}) copy-start(f32[256,256]{1,0:T(8,128)} %param.26) | copy-start | bytes 786436
  136.7 37.9 %collective-permute-start = (bf16[256,256]{1,0:T(8,128)(2,1)S(1)}, bf16[256,256]{1,0:T(8,128)(2,1)S(1)}, u32[]{:S(2)}, u32[]{:S(2)}) collective-permute-start(bf16[256,256]{1,0:T(8,128)(2,1)S(1)} %get-tuple-element.35), channel_id=1, source_target_pairs={{0,4},{4,8},{8,12},{12,0},{1,5},{5,9},{9,13},{13,1},{2,6},{6,10},{... | collective-permute-start | bytes 393224 | tf_op jit(solution)/shard_map/ppermute | solution.py:16
  136.7 54.6 %collective-permute-start.2 = (bf16[256,256]{1,0:T(8,128)(2,1)S(1)}, bf16[256,256]{1,0:T(8,128)(2,1)S(1)}, u32[]{:S(2)}, u32[]{:S(2)}) collective-permute-start(bf16[256,256]{1,0:T(8,128)(2,1)S(1)} %get-tuple-element.35), channel_id=1, source_target_pairs={{0,12},{4,0},{8,4},{12,8},{1,13},{5,1},{9,5},{13,9},{2,14},{6,2},{... | collective-permute-start | bytes 393224 | tf_op jit(solution)/shard_map/ppermute | solution.py:18
  141.4 15.2 %copy-start.5 = (f32[256,256]{1,0:T(8,128)S(1)}, f32[256,256]{1,0:T(8,128)}, u32[]{:S(2)}) copy-start(f32[256,256]{1,0:T(8,128)} %reduce-scatter.9.cloned.1.call-done) | copy-start | bytes 786436
  141.4 15.3 %copy-start.10 = (f32[256,256]{1,0:T(8,128)S(1)}, f32[256,256]{1,0:T(8,128)}, u32[]{:S(2)}) copy-start(f32[256,256]{1,0:T(8,128)} %param.27) | copy-start | bytes 786436
  157.6 16.1 %copy-start.4 = (f32[256,256]{1,0:T(8,128)S(1)}, f32[256,256]{1,0:T(8,128)}, u32[]{:S(2)}) copy-start(f32[256,256]{1,0:T(8,128)} %reduce-scatter.11.cloned.1.call-done) | copy-start | bytes 786436
  157.6 16.1 %copy-start.11 = (f32[256,256]{1,0:T(8,128)S(1)}, f32[256,256]{1,0:T(8,128)}, u32[]{:S(2)}) copy-start(f32[256,256]{1,0:T(8,128)} %param.28) | copy-start | bytes 786436
  174.6 16.6 %collective-permute-start.1 = (bf16[256,256]{1,0:T(8,128)(2,1)S(1)}, bf16[256,256]{1,0:T(8,128)(2,1)S(1)}, u32[]{:S(2)}, u32[]{:S(2)}) collective-permute-start(bf16[256,256]{1,0:T(8,128)(2,1)S(1)} %collective-permute-done), channel_id=1, source_target_pairs={{0,4},{4,8},{8,12},{12,0},{1,5},{5,9},{9,13},{13,1},{2,6},{6,10},{... | collective-permute-start | bytes 393224 | tf_op jit(solution)/shard_map/ppermute | solution.py:16
Sparse Core Ops, SparseCore 0:
  10.3 30.1 reduce-scatter.8
  42.7 25.7 reduce-scatter.10
  70.9 25.7 reduce-scatter.4
  98.8 25.7 reduce-scatter.6
